TPU v7x, 32 devices: a whole 2x2x4 slice. The times are simulated.
32 devices in a mesh: band: 8 (over z, y), feat: 4 (over x, core).
Axes of the slice: x: 2, y: 2, z: 4, core: 2. Of those that a mesh axis runs over, the one named last changes fastest.
Arguments:
- grid_latent: bfloat16 [16384, 512], P('band', 'feat'), may hold values from -6 to 6
- mesh_latent: bfloat16 [1280, 512], P('band', 'feat'), may hold values from -6 to 6
- edge_latent: bfloat16 [8, 4, 2048, 512], P('band', 'feat'), may hold values from -6 to 6
- edge_src: int32 [8, 8192], P('band'), may hold values from 0 to 2047
- edge_dst: int32 [8, 4, 2048], P('band', 'feat'), may hold values from 0 to 160, as said below
- edge_w1: bfloat16 [1536, 512], replicated, may hold values from -0.15625 to 0.15625
- edge_b1: float32 [512], replicated, may hold values from -3 to 3
- edge_w2: bfloat16 [512, 512], replicated, may hold values from -0.25 to 0.25
- edge_b2: float32 [512], replicated, may hold values from -2 to 2
- edge_gain: float32 [512], replicated, may hold values from 0.25 to 1.75
- edge_shift: float32 [512], replicated, may hold values from -2 to 2
- node_w1: bfloat16 [1024, 512], replicated, may hold values from -0.1875 to 0.1875
- node_b1: float32 [512], replicated, may hold values from -3 to 3
- node_w2: bfloat16 [512, 512], replicated, may hold values from -0.25 to 0.25
- node_b2: float32 [512], replicated, may hold values from -2 to 2
- node_gain: float32 [512], replicated, may hold values from 0.25 to 1.75
- node_shift: float32 [512], replicated, may hold values from -2 to 2
Outputs:
- mesh_new: bfloat16 [1280, 512], P('band', 'feat')
Inputs may be any that keep to these rules, and one draw needn't show every extreme that they name: `edge_src`: entry [s, d * 1024 + j] is the grid row, counted within band index s, that sends slot j of the edges from band index s to band index d; empty slots hold some row too. `edge_dst`: entry [d, f, s * 256 + q] is the mesh node, counted within band index d, that receives slot f * 256 + q of the edges from band index s to band index d, or 160 where that slot is empty. The used slots of a pair come first; a pair has at most 1024 used slots. Each receiving band index d hears only from the sending band indices of one latitude span of consecutive indices (edges are local), which lies anywhere along band since mesh partitions are face-major; other pairs are empty. In every draw some band indices receive 1024 from every band index of their span.
All inputs are finite; a program needn't handle non-finite values.
Results may differ from a plain program's by a relative error of at most 0.011.
Values may be sent and summed in bfloat16 or wider, within the bound.
A program may use at most 64 MiB of HBM per device.

v0:
```python
import math
import jax
import jax.numpy as jnp
from jax import lax
from jax.sharding import PartitionSpec as P

EPSILON = 1e-05


def normalize(values, norm_gain, norm_shift):
    average = jnp.mean(values, -1, keepdims=True)
    centered = values - average
    variance = jnp.mean(centered * centered, -1, keepdims=True)
    return centered * lax.rsqrt(variance + EPSILON) * norm_gain + norm_shift


def node_step(row_block, summed, node_w1, node_b1, node_w2, node_b2, node_gain, node_shift):
    full_width = row_block.shape[1]
    hidden = jnp.dot(row_block, node_w1[:full_width], preferred_element_type=jnp.float32)
    hidden = (
        hidden
        + jnp.dot(
            summed.astype(jnp.bfloat16), node_w1[full_width:], preferred_element_type=jnp.float32
        )
        + node_b1
    )
    active = jax.nn.silu(hidden).astype(jnp.bfloat16)
    update = jnp.dot(active, node_w2, preferred_element_type=jnp.float32) + node_b2
    return (row_block.astype(jnp.float32) + normalize(update, node_gain, node_shift)).astype(
        jnp.bfloat16
    )


def select_rows(table, indices):
    total = indices.shape[0]
    block_rows = math.gcd(total, 512)
    grouped = indices.reshape(total // block_rows, block_rows)

    def one_block(block_ids):
        row_ids = lax.broadcasted_iota(jnp.int32, (block_rows, table.shape[0]), 1)
        onehot = (row_ids == block_ids[:, None]).astype(table.dtype)
        return jnp.dot(onehot, table, preferred_element_type=jnp.float32).astype(table.dtype)

    return lax.map(one_block, grouped).reshape(total, table.shape[1])


def body(
    grid_latent,
    mesh_latent,
    edge_latent,
    edge_src,
    edge_dst,
    edge_w1,
    edge_b1,
    edge_w2,
    edge_b2,
    edge_gain,
    edge_shift,
    node_w1,
    node_b1,
    node_w2,
    node_b2,
    node_gain,
    node_shift,
):
    band_count = lax.axis_size("band")
    feat_count = lax.axis_size("feat")
    quarter = grid_latent.shape[1]
    full_width = quarter * feat_count
    mesh_count = mesh_latent.shape[0]
    picked = select_rows(grid_latent, edge_src.reshape(-1)).reshape(band_count, -1, quarter)
    regrouped = lax.all_to_all(picked, "feat", split_axis=1, concat_axis=2, tiled=True)
    arrived = lax.all_to_all(regrouped, "band", split_axis=0, concat_axis=0, tiled=True)
    senders = arrived.reshape(-1, full_width)
    own_edges = edge_latent.reshape(-1, full_width)
    targets = edge_dst.reshape(-1)
    recv_weight = edge_w1[2 * full_width :]
    portion = lax.all_gather(mesh_latent, "feat", axis=1, tiled=True)
    projected = jnp.dot(portion, recv_weight, preferred_element_type=jnp.float32)
    node_ids = lax.broadcasted_iota(jnp.int32, (mesh_count, targets.shape[0]), 0)
    clipped = jnp.minimum(targets, mesh_count - 1)
    pick_node = (node_ids == clipped[None, :]).astype(jnp.float32)
    receiver_part = lax.dot_general(
        pick_node,
        projected,
        (((0,), (0,)), ((), ())),
        precision=lax.Precision.HIGHEST,
        preferred_element_type=jnp.float32,
    )
    hidden = jnp.dot(own_edges, edge_w1[:full_width], preferred_element_type=jnp.float32)
    hidden = hidden + jnp.dot(
        senders, edge_w1[full_width : 2 * full_width], preferred_element_type=jnp.float32
    )
    hidden = hidden + receiver_part + edge_b1
    active = jax.nn.silu(hidden).astype(jnp.bfloat16)
    update = jnp.dot(active, edge_w2, preferred_element_type=jnp.float32) + edge_b2
    edge_new = (own_edges.astype(jnp.float32) + normalize(update, edge_gain, edge_shift)).astype(
        jnp.bfloat16
    )
    selector = (node_ids == targets[None, :]).astype(jnp.bfloat16)
    partial_sums = jnp.dot(selector, edge_new, preferred_element_type=jnp.float32)
    summed = lax.psum(partial_sums.astype(jnp.bfloat16), "feat").astype(jnp.float32)
    updated = node_step(portion, summed, node_w1, node_b1, node_w2, node_b2, node_gain, node_shift)
    own_cols = lax.dynamic_slice_in_dim(updated, lax.axis_index("feat") * quarter, quarter, 1)
    return own_cols


def solution(mesh):
    placed = (
        P("band", "feat"),
        P("band", "feat"),
        P("band", "feat", None, None),
        P("band", None),
        P("band", "feat", None),
        P(),
        P(),
        P(),
        P(),
        P(),
        P(),
        P(),
        P(),
        P(),
        P(),
        P(),
        P(),
    )
    return jax.shard_map(
        body, mesh=mesh, in_specs=placed, out_specs=P("band", "feat"), check_vma=False
    )
```

profile of v0, /device:TPU:0, one launch (start us, length us, event | category | flops | bytes accessed | tf_op | source)
XLA Modules:
  0.0 183.7 jit_solution(7006882849579234291)
XLA Ops:
  7.0 1.4 reduce.3
  8.5 31.7 %while.10 = (s32[]{:T(128)}, bf16[16,512,128]{2,1,0:T(8,128)(2,1)S(1)}, s32[16,512]{1,0:T(8,128)S(1)}, bf16[2048,128]{1,0:T(8,128)(2,1)}, s32[]{:T(128)}) while((s32[]{:T(128)}, bf16[16,512,128]{2,1,0:T(8,128)(2,1)S(1)}, s32[16,512]{1,0:T(8,128)S(1)}, bf16[2048,128]{1,0:T(8,128)(2,1)}, s32[]{:T(128)}) %tuple.21), condition=%wide.region_1.2_spmd, body=%wide.region_0.1_spmd.sunk | while | flops 269549568 | bytes 661573 | solution.py:44
  8.5 1.9 %fusion.46 = bf16[16,512,128]{2,1,0:T(8,128)(2,1)S(1)} fusion(bf16[16,512,128]{2,1,0:T(8,128)(2,1)S(1)} %get-tuple-element.73, s32[]{:T(128)} %get-tuple-element.72, bf16[2048,128]{1,0:T(8,128)(2,1)} %get-tuple-element.80, s32[512]{0:T(512)S(1)} %bitcast.39), kind=kOutput, calls=%fused_computation.5.clone.1 | convolution fusion | flops 269549568 | bytes 657412 | tf_op jit(solution)/shard_map/while/body/eval_jaxpr/dot_general | solution.py:42
  10.5 1.9 %fusion.46 = bf16[16,512,128]{2,1,0:T(8,128)(2,1)S(1)} fusion(bf16[16,512,128]{2,1,0:T(8,128)(2,1)S(1)} %get-tuple-element.73, s32[]{:T(128)} %get-tuple-element.72, bf16[2048,128]{1,0:T(8,128)(2,1)} %get-tuple-element.80, s32[512]{0:T(512)S(1)} %bitcast.39), kind=kOutput, calls=%fused_computation.5.clone.1 | convolution fusion | flops 269549568 | bytes 657412 | tf_op jit(solution)/shard_map/while/body/eval_jaxpr/dot_general | solution.py:42
  12.4 1.9 %fusion.46 = bf16[16,512,128]{2,1,0:T(8,128)(2,1)S(1)} fusion(bf16[16,512,128]{2,1,0:T(8,128)(2,1)S(1)} %get-tuple-element.73, s32[]{:T(128)} %get-tuple-element.72, bf16[2048,128]{1,0:T(8,128)(2,1)} %get-tuple-element.80, s32[512]{0:T(512)S(1)} %bitcast.39), kind=kOutput, calls=%fused_computation.5.clone.1 | convolution fusion | flops 269549568 | bytes 657412 | tf_op jit(solution)/shard_map/while/body/eval_jaxpr/dot_general | solution.py:42
  14.4 1.9 %fusion.46 = bf16[16,512,128]{2,1,0:T(8,128)(2,1)S(1)} fusion(bf16[16,512,128]{2,1,0:T(8,128)(2,1)S(1)} %get-tuple-element.73, s32[]{:T(128)} %get-tuple-element.72, bf16[2048,128]{1,0:T(8,128)(2,1)} %get-tuple-element.80, s32[512]{0:T(512)S(1)} %bitcast.39), kind=kOutput, calls=%fused_computation.5.clone.1 | convolution fusion | flops 269549568 | bytes 657412 | tf_op jit(solution)/shard_map/while/body/eval_jaxpr/dot_general | solution.py:42
  16.4 1.9 %fusion.46 = bf16[16,512,128]{2,1,0:T(8,128)(2,1)S(1)} fusion(bf16[16,512,128]{2,1,0:T(8,128)(2,1)S(1)} %get-tuple-element.73, s32[]{:T(128)} %get-tuple-element.72, bf16[2048,128]{1,0:T(8,128)(2,1)} %get-tuple-element.80, s32[512]{0:T(512)S(1)} %bitcast.39), kind=kOutput, calls=%fused_computation.5.clone.1 | convolution fusion | flops 269549568 | bytes 657412 | tf_op jit(solution)/shard_map/while/body/eval_jaxpr/dot_general | solution.py:42
  18.4 1.9 %fusion.46 = bf16[16,512,128]{2,1,0:T(8,128)(2,1)S(1)} fusion(bf16[16,512,128]{2,1,0:T(8,128)(2,1)S(1)} %get-tuple-element.73, s32[]{:T(128)} %get-tuple-element.72, bf16[2048,128]{1,0:T(8,128)(2,1)} %get-tuple-element.80, s32[512]{0:T(512)S(1)} %bitcast.39), kind=kOutput, calls=%fused_computation.5.clone.1 | convolution fusion | flops 269549568 | bytes 657412 | tf_op jit(solution)/shard_map/while/body/eval_jaxpr/dot_general | solution.py:42
  20.4 1.9 %fusion.46 = bf16[16,512,128]{2,1,0:T(8,128)(2,1)S(1)} fusion(bf16[16,512,128]{2,1,0:T(8,128)(2,1)S(1)} %get-tuple-element.73, s32[]{:T(128)} %get-tuple-element.72, bf16[2048,128]{1,0:T(8,128)(2,1)} %get-tuple-element.80, s32[512]{0:T(512)S(1)} %bitcast.39), kind=kOutput, calls=%fused_computation.5.clone.1 | convolution fusion | flops 269549568 | bytes 657412 | tf_op jit(solution)/shard_map/while/body/eval_jaxpr/dot_general | solution.py:42
  22.3 1.9 %fusion.46 = bf16[16,512,128]{2,1,0:T(8,128)(2,1)S(1)} fusion(bf16[16,512,128]{2,1,0:T(8,128)(2,1)S(1)} %get-tuple-element.73, s32[]{:T(128)} %get-tuple-element.72, bf16[2048,128]{1,0:T(8,128)(2,1)} %get-tuple-element.80, s32[512]{0:T(512)S(1)} %bitcast.39), kind=kOutput, calls=%fused_computation.5.clone.1 | convolution fusion | flops 269549568 | bytes 657412 | tf_op jit(solution)/shard_map/while/body/eval_jaxpr/dot_general | solution.py:42
  24.3 1.9 %fusion.46 = bf16[16,512,128]{2,1,0:T(8,128)(2,1)S(1)} fusion(bf16[16,512,128]{2,1,0:T(8,128)(2,1)S(1)} %get-tuple-element.73, s32[]{:T(128)} %get-tuple-element.72, bf16[2048,128]{1,0:T(8,128)(2,1)} %get-tuple-element.80, s32[512]{0:T(512)S(1)} %bitcast.39), kind=kOutput, calls=%fused_computation.5.clone.1 | convolution fusion | flops 269549568 | bytes 657412 | tf_op jit(solution)/shard_map/while/body/eval_jaxpr/dot_general | solution.py:42
  26.3 1.9 %fusion.46 = bf16[16,512,128]{2,1,0:T(8,128)(2,1)S(1)} fusion(bf16[16,512,128]{2,1,0:T(8,128)(2,1)S(1)} %get-tuple-element.73, s32[]{:T(128)} %get-tuple-element.72, bf16[2048,128]{1,0:T(8,128)(2,1)} %get-tuple-element.80, s32[512]{0:T(512)S(1)} %bitcast.39), kind=kOutput, calls=%fused_computation.5.clone.1 | convolution fusion | flops 269549568 | bytes 657412 | tf_op jit(solution)/shard_map/while/body/eval_jaxpr/dot_general | solution.py:42
  28.3 1.9 %fusion.46 = bf16[16,512,128]{2,1,0:T(8,128)(2,1)S(1)} fusion(bf16[16,512,128]{2,1,0:T(8,128)(2,1)S(1)} %get-tuple-element.73, s32[]{:T(128)} %get-tuple-element.72, bf16[2048,128]{1,0:T(8,128)(2,1)} %get-tuple-element.80, s32[512]{0:T(512)S(1)} %bitcast.39), kind=kOutput, calls=%fused_computation.5.clone.1 | convolution fusion | flops 269549568 | bytes 657412 | tf_op jit(solution)/shard_map/while/body/eval_jaxpr/dot_general | solution.py:42
  30.3 1.9 %fusion.46 = bf16[16,512,128]{2,1,0:T(8,128)(2,1)S(1)} fusion(bf16[16,512,128]{2,1,0:T(8,128)(2,1)S(1)} %get-tuple-element.73, s32[]{:T(128)} %get-tuple-element.72, bf16[2048,128]{1,0:T(8,128)(2,1)} %get-tuple-element.80, s32[512]{0:T(512)S(1)} %bitcast.39), kind=kOutput, calls=%fused_computation.5.clone.1 | convolution fusion | flops 269549568 | bytes 657412 | tf_op jit(solution)/shard_map/while/body/eval_jaxpr/dot_general | solution.py:42
  32.2 1.9 %fusion.46 = bf16[16,512,128]{2,1,0:T(8,128)(2,1)S(1)} fusion(bf16[16,512,128]{2,1,0:T(8,128)(2,1)S(1)} %get-tuple-element.73, s32[]{:T(128)} %get-tuple-element.72, bf16[2048,128]{1,0:T(8,128)(2,1)} %get-tuple-element.80, s32[512]{0:T(512)S(1)} %bitcast.39), kind=kOutput, calls=%fused_computation.5.clone.1 | convolution fusion | flops 269549568 | bytes 657412 | tf_op jit(solution)/shard_map/while/body/eval_jaxpr/dot_general | solution.py:42
  34.2 1.9 %fusion.46 = bf16[16,512,128]{2,1,0:T(8,128)(2,1)S(1)} fusion(bf16[16,512,128]{2,1,0:T(8,128)(2,1)S(1)} %get-tuple-element.73, s32[]{:T(128)} %get-tuple-element.72, bf16[2048,128]{1,0:T(8,128)(2,1)} %get-tuple-element.80, s32[512]{0:T(512)S(1)} %bitcast.39), kind=kOutput, calls=%fused_computation.5.clone.1 | convolution fusion | flops 269549568 | bytes 657412 | tf_op jit(solution)/shard_map/while/body/eval_jaxpr/dot_general | solution.py:42
  36.2 1.9 %fusion.46 = bf16[16,512,128]{2,1,0:T(8,128)(2,1)S(1)} fusion(bf16[16,512,128]{2,1,0:T(8,128)(2,1)S(1)} %get-tuple-element.73, s32[]{:T(128)} %get-tuple-element.72, bf16[2048,128]{1,0:T(8,128)(2,1)} %get-tuple-element.80, s32[512]{0:T(512)S(1)} %bitcast.39), kind=kOutput, calls=%fused_computation.5.clone.1 | convolution fusion | flops 269549568 | bytes 657412 | tf_op jit(solution)/shard_map/while/body/eval_jaxpr/dot_general | solution.py:42
  38.2 1.9 %fusion.46 = bf16[16,512,128]{2,1,0:T(8,128)(2,1)S(1)} fusion(bf16[16,512,128]{2,1,0:T(8,128)(2,1)S(1)} %get-tuple-element.73, s32[]{:T(128)} %get-tuple-element.72, bf16[2048,128]{1,0:T(8,128)(2,1)} %get-tuple-element.80, s32[512]{0:T(512)S(1)} %bitcast.39), kind=kOutput, calls=%fused_computation.5.clone.1 | convolution fusion | flops 269549568 | bytes 657412 | tf_op jit(solution)/shard_map/while/body/eval_jaxpr/dot_general | solution.py:42
  41.5 29.8 %all_to_all.23 = bf16[8,1024,128]{2,0,1:T(8,128)(2,1)} all-to-all(bf16[8,1024,128]{2,0,1:T(8,128)(2,1)S(1)} %copy.28), channel_id=1, replica_groups=mesh['band'=8,'feat'=4] {'feat'}, dimensions={1} | all-to-all | bytes 4194304 | tf_op jit(solution)/shard_map/all_to_all | solution.py:72
  71.3 4.5 %copy.30 = bf16[8,256,4,128]{1,3,2,0:T(8,128)(2,1)} copy(bf16[8,256,4,128]{3,0,1,2:T(8,128)(2,1)} %bitcast.37) | data formatting | bytes 4194304 | tf_op jit(solution)/shard_map/all_to_all | solution.py:72
  75.8 6.5 %all-to-all-start.1 = ((bf16[8,256,512]{1,2,0:T(8,128)(2,1)}), bf16[8,256,512]{1,2,0:T(8,128)(2,1)}, u32[]{:S(2)}, u32[]{:S(2)}) async-start(bf16[8,256,512]{1,2,0:T(8,128)(2,1)} %bitcast.36), calls=%async_computation.1 | async-start | bytes 4194304 | tf_op jit(solution)/shard_map/all_to_all | solution.py:73
  82.3 2.5 %copy.27 = bf16[1,1,2048,512]{2,3,1,0:T(8,128)(2,1)} copy(bf16[1,1,2048,512]{3,2,1,0:T(8,128)(2,1)S(1)} %copy-done.1) | data formatting | bytes 4194304 | tf_op args[2]
  84.8 5.7 %all_gather.3 = bf16[160,512]{1,0:T(8,128)(2,1)S(1)} all-gather(bf16[160,128]{1,0:T(8,128)(2,1)S(1)} %copy-done.5), channel_id=1, replica_groups=mesh['band'=8,'feat'=4] {'feat'}, dimensions={1}, use_global_device_ids=true | all-gather | bytes 204800 | tf_op jit(solution)/shard_map/all_gather | solution.py:78
  91.8 4.2 %fusion.5 = f32[2048,512]{1,0:T(8,128)} fusion(bf16[1,1,2048,512]{3,2,1,0:T(8,128)(2,1)S(1)} %copy-done.1, bf16[1536,512]{1,0:T(8,128)(2,1)} %param.24), kind=kOutput, calls=%fused_computation.11 | convolution fusion | flops 1073741824 | bytes 6815744 | tf_op jit(solution)/shard_map/dot_general | solution.py:90
  96.1 34.2 %all-to-all-done.1 = bf16[8,256,512]{1,2,0:T(8,128)(2,1)} async-done(((bf16[8,256,512]{1,2,0:T(8,128)(2,1)}), bf16[8,256,512]{1,2,0:T(8,128)(2,1)}, u32[]{:S(2)}, u32[]{:S(2)}) %all-to-all-start.1) | async-done | bytes 2097184 | tf_op jit(solution)/shard_map/all_to_all | solution.py:73
  130.3 2.9 %copy.31 = bf16[8,256,512]{2,1,0:T(8,128)(2,1)S(1)} copy(bf16[8,256,512]{1,2,0:T(8,128)(2,1)} %all-to-all-done.1) | data formatting | bytes 4194304 | tf_op jit(solution)/shard_map/all_to_all | solution.py:73
  133.2 2.4 %fusion.15 = f32[2048,512]{1,0:T(8,128)S(1)} fusion(bf16[2048,512]{1,0:T(8,128)(2,1)S(1)} %bitcast.35, bf16[1536,512]{1,0:T(8,128)(2,1)} %param.24), kind=kOutput, calls=%fused_computation.25 | convolution fusion | flops 1073741824 | bytes 6815744 | tf_op jit(solution)/shard_map/dot_general | solution.py:91
  135.6 3.0 %multiply_convert_fusion = bf16[2048,512]{1,0:T(8,128)(2,1)S(1)} fusion(f32[2048,512]{1,0:T(8,128)S(1)} %copy-done.2, f32[2048,512]{1,0:T(8,128)S(1)} %fusion.15, f32[160,512]{1,0:T(8,128)S(1)} %fusion.13, f32[512]{0:T(512)S(1)} %copy-done.9, s32[2048]{0:T(1024)S(1)} %broadcast_minimum_fusion), kind=kOutput, calls=%fused_computation.9 | convolution fusion | flops 2021982208 | bytes 10823680 | tf_op jit(solution)/shard_map/dot_general | solution.py:83
  138.7 1.4 add_reduce_fusion
  141.7 2.3 %fusion.9 = bf16[160,512]{1,0:T(8,128)(2,1)} fusion(f32[2048,512]{0,1:T(8,128)S(1)} %get-tuple-element.39, bf16[1,1,2048,512]{2,3,1,0:T(8,128)(2,1)S(1)} %copy-done.3, f32[512]{0:T(512)S(1)} %copy-done.10, f32[512]{0:T(512)S(1)} %copy-done.11, f32[2048]{0:T(1024)S(1)} %add_rsqrt_fusion, f32[2048]{0:T(1024)S(1)} %broadcast_multiply_fusion, ...), kind=kOutput, calls=%fused_computation.19 | convolution fusion | flops 344342528 | bytes 6486016 | tf_op jit(solution)/shard_map/dot_general | solution.py:101
  145.7 28.6 %all-reduce.2.cloned.1.call-done = bf16[160,512]{1,0:T(8,128)(2,1)} async-done(((bf16[160,512]{1,0:T(8,128)(2,1)}), bf16[160,512]{1,0:T(8,128)(2,1)}) %all-reduce.2.cloned.1.call-update) | async-done | bytes 163856 | tf_op jit(solution)/shard_map/psum | solution.py:102
  174.4 1.5 fusion.31
  (62 shorter events, 7.7 us)
Async XLA Ops:
  6.5 132.1 %copy-start = (bf16[512,512]{1,0:T(8,128)(2,1)S(1)}, bf16[512,512]{1,0:T(8,128)(2,1)}, u32[]{:S(2)}) copy-start(bf16[512,512]{1,0:T(8,128)(2,1)} %param.26) | copy-start | bytes 1572868
  71.3 11.0 %copy-start.1 = (bf16[1,1,2048,512]{3,2,1,0:T(8,128)(2,1)S(1)}, bf16[1,1,2048,512]{3,2,1,0:T(8,128)(2,1)}, u32[]{:S(2)}) copy-start(bf16[1,1,2048,512]{3,2,1,0:T(8,128)(2,1)} %param.21) | copy-start | bytes 6291460
  75.8 9.1 %copy-start.5 = (bf16[160,128]{1,0:T(8,128)(2,1)S(1)}, bf16[160,128]{1,0:T(8,128)(2,1)}, u32[]{:S(2)}) copy-start(bf16[160,128]{1,0:T(8,128)(2,1)} %param.20) | copy-start | bytes 122884
  75.8 14.8 %copy-start.6 = (s32[1,1,2048]{2,1,0:T(1,128)S(1)}, s32[1,1,2048]{2,1,0:T(1,128)}, u32[]{:S(2)}) copy-start(s32[1,1,2048]{2,1,0:T(1,128)} %param.23) | copy-start | bytes 24580
  75.8 54.5 %all-to-all-start.1 = ((bf16[8,256,512]{1,2,0:T(8,128)(2,1)}), bf16[8,256,512]{1,2,0:T(8,128)(2,1)}, u32[]{:S(2)}, u32[]{:S(2)}) async-start(bf16[8,256,512]{1,2,0:T(8,128)(2,1)} %bitcast.36), calls=%async_computation.1 | async-start | bytes 4194304 | tf_op jit(solution)/shard_map/all_to_all | solution.py:73
  82.3 92.1 %all-reduce.2.cloned.1.call-start = ((), (), s32[]{:S(2)}) async-start(), calls=%async_computation.2 | async-start | bytes 327680 | tf_op jit(solution)/shard_map/psum | solution.py:102
  133.1 2.5 %copy-start.2 = (f32[2048,512]{1,0:T(8,128)S(1)}, f32[2048,512]{1,0:T(8,128)}, u32[]{:S(2)}) copy-start(f32[2048,512]{1,0:T(8,128)} %fusion.5) | copy-start | bytes 12582916
  133.1 2.5 %copy-start.9 = (f32[512]{0:T(512)S(1)}, f32[512]{0:T(512)}, u32[]{:S(2)}) copy-start(f32[512]{0:T(512)} %param.25) | copy-start | bytes 6148
  135.6 3.0 %copy-start.7 = (f32[512]{0:T(512)S(1)}, f32[512]{0:T(512)}, u32[]{:S(2)}) copy-start(f32[512]{0:T(512)} %param.27) | copy-start | bytes 6148
  140.0 1.6 copy-start.3
  140.1 1.6 copy-start.10
  140.1 1.6 copy-start.11
  141.6 2.3 %copy-start.4 = (bf16[1024,512]{1,0:T(8,128)(2,1)S(1)}, bf16[1024,512]{1,0:T(8,128)(2,1)}, u32[]{:S(2)}) copy-start(bf16[1024,512]{1,0:T(8,128)(2,1)} %param.30) | copy-start | bytes 3145732
  141.6 32.7 %copy-start.8 = (bf16[512,512]{1,0:T(8,128)(2,1)S(1)}, bf16[512,512]{1,0:T(8,128)(2,1)}, u32[]{:S(2)}) copy-start(bf16[512,512]{1,0:T(8,128)(2,1)} %param.32) | copy-start | bytes 1572868
  141.6 32.7 %copy-start.12 = (f32[512]{0:T(512)S(1)}, f32[512]{0:T(512)}, u32[]{:S(2)}) copy-start(f32[512]{0:T(512)} %param.33) | copy-start | bytes 6148
  141.7 32.7 %copy-start.13 = (f32[512]{0:T(512)S(1)}, f32[512]{0:T(512)}, u32[]{:S(2)}) copy-start(f32[512]{0:T(512)} %param.31) | copy-start | bytes 6148
Sparse Core Ops, SparseCore 0:
  144.1 30.2 all-reduce.1
where the time goes:
time: 185 us; the launch traced here: 184 us
  waiting for transfers between devices  62.9 us (34%)
  matrix products  47.5 us (26%)
  blocking collectives  35.5 us (19%)
  local copies, waits for them, and re-layouts  14.3 us (8%)
  between operations  13.6 us (7%)
  starting transfers between devices  6.57 us (4%)
  other arithmetic  2.98 us (2%)
    all_to_all x1, waiting for transfers between devices, body(): lax.all_to_all(regrouped, 'band', split_axis=0, concat_axis=0, tiled=True)  34.2 us
    dot_general x16, matrix products, one_block(): jnp.dot(onehot, table, preferred_element_type=jnp.float32)  31.1 us
    all_to_all x1, blocking collectives, body(): lax.all_to_all(picked, 'feat', split_axis=1, concat_axis=2, tiled=True)  29.8 us
    psum x1, waiting for transfers between devices, body(): lax.psum(partial_sums.astype(jnp.bfloat16), 'feat').astype(jnp.float32)  28.6 us
    all_to_all x1, starting transfers between devices, body(): lax.all_to_all(regrouped, 'band', split_axis=0, concat_axis=0, tiled=True)  6.53 us
    all_gather x1, blocking collectives, body(): portion = lax.all_gather(mesh_latent, 'feat', axis=1, tiled=True)  5.7 us
    all_to_all x1, local copies, waits for them, and re-layouts, body(): lax.all_to_all(picked, 'feat', split_axis=1, concat_axis=2, tiled=True)  4.46 us
    dot_general x1, matrix products, body(): jnp.dot(own_edges, edge_w1[:full_width], preferred_element_type=jnp.float32)  4.22 us
  transfers between devices with their start and end apart: 2, of which 2 were waited for; matrix products, arithmetic and copies ran while one was open for 5% of the time, Pallas kernels for 0%

commit v1 on v0

--- a/solution.py
+++ b/solution.py
@@ -5,6 +5,11 @@
 from jax.sharding import PartitionSpec as P
 
 EPSILON = 1e-05
+
+
+def play_patch(unit):
+    built = jnp.sum(lax.all_gather(unit, axis_name="feat"), axis=0)
+    return built
 
 
 def normalize(values, norm_gain, norm_shift):
@@ -99,7 +104,7 @@
     )
     selector = (node_ids == targets[None, :]).astype(jnp.bfloat16)
     partial_sums = jnp.dot(selector, edge_new, preferred_element_type=jnp.float32)
-    summed = lax.psum(partial_sums.astype(jnp.bfloat16), "feat").astype(jnp.float32)
+    summed = play_patch(partial_sums.astype(jnp.bfloat16)).astype(jnp.float32)
     updated = node_step(portion, summed, node_w1, node_b1, node_w2, node_b2, node_gain, node_shift)
     own_cols = lax.dynamic_slice_in_dim(updated, lax.axis_index("feat") * quarter, quarter, 1)
     return own_cols

time: 185 us -> 148 us (0.80)
  waiting for transfers between devices: 62.9 us -> 31.5 us
  between operations: 13.6 us -> 0.22 us
  blocking collectives: 35.5 us -> 42.7 us
    psum x1 -> x0, waiting for transfers between devices: 28.6 us -> none  [body(): lax.psum(partial_sums.astype(jnp.bfloat16), 'feat').astype(jnp.float32)]
    all_gather x0 -> x1, blocking collectives: none -> 7.19 us  [play_patch(): built = jnp.sum(lax.all_gather(unit, axis_name='feat'), axis=0)]
    all_to_all x1, waiting for transfers between devices: 34.2 us -> 31.5 us  [body(): lax.all_to_all(regrouped, 'band', split_axis=0, concat_axis=0, tiled=True)]
    unnamed x30 -> x26, local copies, waits for them, and re-layouts: 3.95 us -> 3.92 us
  transfers between devices with their start and end apart: 2 -> 1, of which waited for: 2 -> 1; matrix products, arithmetic and copies ran while one was open for 5% -> 7% of each run, Pallas kernels for 0% -> 0%
where the time goes in v1:
time: 148 us; the launch traced here: 147 us
  matrix products  48.1 us (32%)
  blocking collectives  42.7 us (29%)
  waiting for transfers between devices  31.5 us (21%)
  local copies, waits for them, and re-layouts  14.3 us (10%)
  starting transfers between devices  6.53 us (4%)
  other arithmetic  3.07 us (2%)
    all_to_all x1, waiting for transfers between devices, body(): lax.all_to_all(regrouped, 'band', split_axis=0, concat_axis=0, tiled=True)  31.5 us
    dot_general x16, matrix products, one_block(): jnp.dot(onehot, table, preferred_element_type=jnp.float32)  31.1 us
    all_to_all x1, blocking collectives, body(): lax.all_to_all(picked, 'feat', split_axis=1, concat_axis=2, tiled=True)  29.8 us
    all_gather x1, blocking collectives, play_patch(): built = jnp.sum(lax.all_gather(unit, axis_name='feat'), axis=0)  7.19 us
    all_to_all x1, starting transfers between devices, body(): lax.all_to_all(regrouped, 'band', split_axis=0, concat_axis=0, tiled=True)  6.53 us
    all_gather x1, blocking collectives, body(): portion = lax.all_gather(mesh_latent, 'feat', axis=1, tiled=True)  5.7 us
    all_to_all x1, local copies, waits for them, and re-layouts, body(): lax.all_to_all(picked, 'feat', split_axis=1, concat_axis=2, tiled=True)  4.51 us
    dot_general x1, matrix products, body(): jnp.dot(own_edges, edge_w1[:full_width], preferred_element_type=jnp.float32)  4.23 us
  transfers between devices with their start and end apart: 1, of which 1 were waited for; matrix products, arithmetic and copies ran while one was open for 7% of the time, Pallas kernels for 0%

profile of v1, /device:TPU:0, one launch (start us, length us, event | category | flops | bytes accessed | tf_op | source)
XLA Modules:
  0.0 146.8 jit_solution(8575531765120464572)
XLA Ops:
  0.5 1.4 reduce.4
  1.9 31.7 %while.10 = (s32[]{:T(128)}, bf16[16,512,128]{2,1,0:T(8,128)(2,1)S(1)}, s32[16,512]{1,0:T(8,128)S(1)}, bf16[2048,128]{1,0:T(8,128)(2,1)}, s32[]{:T(128)}) while((s32[]{:T(128)}, bf16[16,512,128]{2,1,0:T(8,128)(2,1)S(1)}, s32[16,512]{1,0:T(8,128)S(1)}, bf16[2048,128]{1,0:T(8,128)(2,1)}, s32[]{:T(128)}) %tuple.21), condition=%wide.region_1.2_spmd, body=%wide.region_0.1_spmd.sunk | while | flops 269549568 | bytes 661573 | solution.py:49
  1.9 1.9 %fusion.46 = bf16[16,512,128]{2,1,0:T(8,128)(2,1)S(1)} fusion(bf16[16,512,128]{2,1,0:T(8,128)(2,1)S(1)} %get-tuple-element.73, s32[]{:T(128)} %get-tuple-element.72, bf16[2048,128]{1,0:T(8,128)(2,1)} %get-tuple-element.80, s32[512]{0:T(512)S(1)} %bitcast.41), kind=kOutput, calls=%fused_computation.5.clone.1 | convolution fusion | flops 269549568 | bytes 657412 | tf_op jit(solution)/shard_map/while/body/eval_jaxpr/dot_general | solution.py:47
  3.9 1.9 %fusion.46 = bf16[16,512,128]{2,1,0:T(8,128)(2,1)S(1)} fusion(bf16[16,512,128]{2,1,0:T(8,128)(2,1)S(1)} %get-tuple-element.73, s32[]{:T(128)} %get-tuple-element.72, bf16[2048,128]{1,0:T(8,128)(2,1)} %get-tuple-element.80, s32[512]{0:T(512)S(1)} %bitcast.41), kind=kOutput, calls=%fused_computation.5.clone.1 | convolution fusion | flops 269549568 | bytes 657412 | tf_op jit(solution)/shard_map/while/body/eval_jaxpr/dot_general | solution.py:47
  5.9 1.9 %fusion.46 = bf16[16,512,128]{2,1,0:T(8,128)(2,1)S(1)} fusion(bf16[16,512,128]{2,1,0:T(8,128)(2,1)S(1)} %get-tuple-element.73, s32[]{:T(128)} %get-tuple-element.72, bf16[2048,128]{1,0:T(8,128)(2,1)} %get-tuple-element.80, s32[512]{0:T(512)S(1)} %bitcast.41), kind=kOutput, calls=%fused_computation.5.clone.1 | convolution fusion | flops 269549568 | bytes 657412 | tf_op jit(solution)/shard_map/while/body/eval_jaxpr/dot_general | solution.py:47
  7.9 1.9 %fusion.46 = bf16[16,512,128]{2,1,0:T(8,128)(2,1)S(1)} fusion(bf16[16,512,128]{2,1,0:T(8,128)(2,1)S(1)} %get-tuple-element.73, s32[]{:T(128)} %get-tuple-element.72, bf16[2048,128]{1,0:T(8,128)(2,1)} %get-tuple-element.80, s32[512]{0:T(512)S(1)} %bitcast.41), kind=kOutput, calls=%fused_computation.5.clone.1 | convolution fusion | flops 269549568 | bytes 657412 | tf_op jit(solution)/shard_map/while/body/eval_jaxpr/dot_general | solution.py:47
  9.9 1.9 %fusion.46 = bf16[16,512,128]{2,1,0:T(8,128)(2,1)S(1)} fusion(bf16[16,512,128]{2,1,0:T(8,128)(2,1)S(1)} %get-tuple-element.73, s32[]{:T(128)} %get-tuple-element.72, bf16[2048,128]{1,0:T(8,128)(2,1)} %get-tuple-element.80, s32[512]{0:T(512)S(1)} %bitcast.41), kind=kOutput, calls=%fused_computation.5.clone.1 | convolution fusion | flops 269549568 | bytes 657412 | tf_op jit(solution)/shard_map/while/body/eval_jaxpr/dot_general | solution.py:47
  11.8 1.9 %fusion.46 = bf16[16,512,128]{2,1,0:T(8,128)(2,1)S(1)} fusion(bf16[16,512,128]{2,1,0:T(8,128)(2,1)S(1)} %get-tuple-element.73, s32[]{:T(128)} %get-tuple-element.72, bf16[2048,128]{1,0:T(8,128)(2,1)} %get-tuple-element.80, s32[512]{0:T(512)S(1)} %bitcast.41), kind=kOutput, calls=%fused_computation.5.clone.1 | convolution fusion | flops 269549568 | bytes 657412 | tf_op jit(solution)/shard_map/while/body/eval_jaxpr/dot_general | solution.py:47
  13.8 1.9 %fusion.46 = bf16[16,512,128]{2,1,0:T(8,128)(2,1)S(1)} fusion(bf16[16,512,128]{2,1,0:T(8,128)(2,1)S(1)} %get-tuple-element.73, s32[]{:T(128)} %get-tuple-element.72, bf16[2048,128]{1,0:T(8,128)(2,1)} %get-tuple-element.80, s32[512]{0:T(512)S(1)} %bitcast.41), kind=kOutput, calls=%fused_computation.5.clone.1 | convolution fusion | flops 269549568 | bytes 657412 | tf_op jit(solution)/shard_map/while/body/eval_jaxpr/dot_general | solution.py:47
  15.8 1.9 %fusion.46 = bf16[16,512,128]{2,1,0:T(8,128)(2,1)S(1)} fusion(bf16[16,512,128]{2,1,0:T(8,128)(2,1)S(1)} %get-tuple-element.73, s32[]{:T(128)} %get-tuple-element.72, bf16[2048,128]{1,0:T(8,128)(2,1)} %get-tuple-element.80, s32[512]{0:T(512)S(1)} %bitcast.41), kind=kOutput, calls=%fused_computation.5.clone.1 | convolution fusion | flops 269549568 | bytes 657412 | tf_op jit(solution)/shard_map/while/body/eval_jaxpr/dot_general | solution.py:47
  17.8 1.9 %fusion.46 = bf16[16,512,128]{2,1,0:T(8,128)(2,1)S(1)} fusion(bf16[16,512,128]{2,1,0:T(8,128)(2,1)S(1)} %get-tuple-element.73, s32[]{:T(128)} %get-tuple-element.72, bf16[2048,128]{1,0:T(8,128)(2,1)} %get-tuple-element.80, s32[512]{0:T(512)S(1)} %bitcast.41), kind=kOutput, calls=%fused_computation.5.clone.1 | convolution fusion | flops 269549568 | bytes 657412 | tf_op jit(solution)/shard_map/while/body/eval_jaxpr/dot_general | solution.py:47
  19.8 1.9 %fusion.46 = bf16[16,512,128]{2,1,0:T(8,128)(2,1)S(1)} fusion(bf16[16,512,128]{2,1,0:T(8,128)(2,1)S(1)} %get-tuple-element.73, s32[]{:T(128)} %get-tuple-element.72, bf16[2048,128]{1,0:T(8,128)(2,1)} %get-tuple-element.80, s32[512]{0:T(512)S(1)} %bitcast.41), kind=kOutput, calls=%fused_computation.5.clone.1 | convolution fusion | flops 269549568 | bytes 657412 | tf_op jit(solution)/shard_map/while/body/eval_jaxpr/dot_general | solution.py:47
  21.7 1.9 %fusion.46 = bf16[16,512,128]{2,1,0:T(8,128)(2,1)S(1)} fusion(bf16[16,512,128]{2,1,0:T(8,128)(2,1)S(1)} %get-tuple-element.73, s32[]{:T(128)} %get-tuple-element.72, bf16[2048,128]{1,0:T(8,128)(2,1)} %get-tuple-element.80, s32[512]{0:T(512)S(1)} %bitcast.41), kind=kOutput, calls=%fused_computation.5.clone.1 | convolution fusion | flops 269549568 | bytes 657412 | tf_op jit(solution)/shard_map/while/body/eval_jaxpr/dot_general | solution.py:47
  23.7 1.9 %fusion.46 = bf16[16,512,128]{2,1,0:T(8,128)(2,1)S(1)} fusion(bf16[16,512,128]{2,1,0:T(8,128)(2,1)S(1)} %get-tuple-element.73, s32[]{:T(128)} %get-tuple-element.72, bf16[2048,128]{1,0:T(8,128)(2,1)} %get-tuple-element.80, s32[512]{0:T(512)S(1)} %bitcast.41), kind=kOutput, calls=%fused_computation.5.clone.1 | convolution fusion | flops 269549568 | bytes 657412 | tf_op jit(solution)/shard_map/while/body/eval_jaxpr/dot_general | solution.py:47
  25.7 1.9 %fusion.46 = bf16[16,512,128]{2,1,0:T(8,128)(2,1)S(1)} fusion(bf16[16,512,128]{2,1,0:T(8,128)(2,1)S(1)} %get-tuple-element.73, s32[]{:T(128)} %get-tuple-element.72, bf16[2048,128]{1,0:T(8,128)(2,1)} %get-tuple-element.80, s32[512]{0:T(512)S(1)} %bitcast.41), kind=kOutput, calls=%fused_computation.5.clone.1 | convolution fusion | flops 269549568 | bytes 657412 | tf_op jit(solution)/shard_map/while/body/eval_jaxpr/dot_general | solution.py:47
  27.7 1.9 %fusion.46 = bf16[16,512,128]{2,1,0:T(8,128)(2,1)S(1)} fusion(bf16[16,512,128]{2,1,0:T(8,128)(2,1)S(1)} %get-tuple-element.73, s32[]{:T(128)} %get-tuple-element.72, bf16[2048,128]{1,0:T(8,128)(2,1)} %get-tuple-element.80, s32[512]{0:T(512)S(1)} %bitcast.41), kind=kOutput, calls=%fused_computation.5.clone.1 | convolution fusion | flops 269549568 | bytes 657412 | tf_op jit(solution)/shard_map/while/body/eval_jaxpr/dot_general | solution.py:47
  29.7 1.9 %fusion.46 = bf16[16,512,128]{2,1,0:T(8,128)(2,1)S(1)} fusion(bf16[16,512,128]{2,1,0:T(8,128)(2,1)S(1)} %get-tuple-element.73, s32[]{:T(128)} %get-tuple-element.72, bf16[2048,128]{1,0:T(8,128)(2,1)} %get-tuple-element.80, s32[512]{0:T(512)S(1)} %bitcast.41), kind=kOutput, calls=%fused_computation.5.clone.1 | convolution fusion | flops 269549568 | bytes 657412 | tf_op jit(solution)/shard_map/while/body/eval_jaxpr/dot_general | solution.py:47
  31.6 1.9 %fusion.46 = bf16[16,512,128]{2,1,0:T(8,128)(2,1)S(1)} fusion(bf16[16,512,128]{2,1,0:T(8,128)(2,1)S(1)} %get-tuple-element.73, s32[]{:T(128)} %get-tuple-element.72, bf16[2048,128]{1,0:T(8,128)(2,1)} %get-tuple-element.80, s32[512]{0:T(512)S(1)} %bitcast.41), kind=kOutput, calls=%fused_computation.5.clone.1 | convolution fusion | flops 269549568 | bytes 657412 | tf_op jit(solution)/shard_map/while/body/eval_jaxpr/dot_general | solution.py:47
  35.0 29.8 %all_to_all.23 = bf16[8,1024,128]{2,0,1:T(8,128)(2,1)} all-to-all(bf16[8,1024,128]{2,0,1:T(8,128)(2,1)S(1)} %copy.28), channel_id=1, replica_groups=mesh['band'=8,'feat'=4] {'feat'}, dimensions={1} | all-to-all | bytes 4194304 | tf_op jit(solution)/shard_map/all_to_all | solution.py:77
  64.8 4.5 %copy.30 = bf16[8,256,4,128]{1,3,2,0:T(8,128)(2,1)} copy(bf16[8,256,4,128]{3,0,1,2:T(8,128)(2,1)} %bitcast.38) | data formatting | bytes 4194304 | tf_op jit(solution)/shard_map/all_to_all | solution.py:77
  69.3 6.5 %all-to-all-start.1 = ((bf16[8,256,512]{1,2,0:T(8,128)(2,1)}), bf16[8,256,512]{1,2,0:T(8,128)(2,1)}, u32[]{:S(2)}, u32[]{:S(2)}) async-start(bf16[8,256,512]{1,2,0:T(8,128)(2,1)} %bitcast.37), calls=%async_computation.1 | async-start | bytes 4194304 | tf_op jit(solution)/shard_map/all_to_all | solution.py:78
  75.8 2.5 %copy.27 = bf16[1,1,2048,512]{2,3,1,0:T(8,128)(2,1)} copy(bf16[1,1,2048,512]{3,2,1,0:T(8,128)(2,1)S(1)} %copy-done.1) | data formatting | bytes 4194304 | tf_op args[2]
  79.8 5.7 %all_gather.9 = bf16[160,512]{1,0:T(8,128)(2,1)S(1)} all-gather(bf16[160,128]{1,0:T(8,128)(2,1)S(1)} %copy-done.4), channel_id=1, replica_groups=mesh['band'=8,'feat'=4] {'feat'}, dimensions={1}, use_global_device_ids=true | all-gather | bytes 204800 | tf_op jit(solution)/shard_map/all_gather | solution.py:83
  88.1 4.2 %fusion.5 = f32[2048,512]{1,0:T(8,128)} fusion(bf16[1,1,2048,512]{3,2,1,0:T(8,128)(2,1)S(1)} %copy-done.1, bf16[1536,512]{1,0:T(8,128)(2,1)} %param.24), kind=kOutput, calls=%fused_computation.11 | convolution fusion | flops 1073741824 | bytes 6815744 | tf_op jit(solution)/shard_map/dot_general | solution.py:95
  92.3 31.5 %all-to-all-done.1 = bf16[8,256,512]{1,2,0:T(8,128)(2,1)} async-done(((bf16[8,256,512]{1,2,0:T(8,128)(2,1)}), bf16[8,256,512]{1,2,0:T(8,128)(2,1)}, u32[]{:S(2)}, u32[]{:S(2)}) %all-to-all-start.1) | async-done | bytes 2097184 | tf_op jit(solution)/shard_map/all_to_all | solution.py:78
  123.8 2.9 %copy.31 = bf16[8,256,512]{2,1,0:T(8,128)(2,1)S(1)} copy(bf16[8,256,512]{1,2,0:T(8,128)(2,1)} %all-to-all-done.1) | data formatting | bytes 4194304 | tf_op jit(solution)/shard_map/all_to_all | solution.py:78
  126.7 2.4 %fusion.15 = f32[2048,512]{1,0:T(8,128)S(1)} fusion(bf16[2048,512]{1,0:T(8,128)(2,1)S(1)} %bitcast.36, bf16[1536,512]{1,0:T(8,128)(2,1)} %param.24), kind=kOutput, calls=%fused_computation.25 | convolution fusion | flops 1073741824 | bytes 6815744 | tf_op jit(solution)/shard_map/dot_general | solution.py:96
  129.1 3.0 %multiply_convert_fusion = bf16[2048,512]{1,0:T(8,128)(2,1)S(1)} fusion(f32[2048,512]{1,0:T(8,128)S(1)} %copy-done.2, f32[2048,512]{1,0:T(8,128)S(1)} %fusion.15, f32[160,512]{1,0:T(8,128)S(1)} %fusion.13, f32[512]{0:T(512)S(1)} %copy-done.7, s32[2048]{0:T(1024)S(1)} %broadcast_minimum_fusion), kind=kOutput, calls=%fused_computation.9 | convolution fusion | flops 2021982208 | bytes 10823680 | tf_op jit(solution)/shard_map/dot_general | solution.py:88
  132.2 1.4 add_reduce_fusion
  135.2 1.6 %fusion.9 = bf16[160,512]{1,0:T(8,128)(2,1)S(1)} fusion(f32[2048,512]{0,1:T(8,128)S(1)} %get-tuple-element.39, bf16[1,1,2048,512]{2,3,1,0:T(8,128)(2,1)S(1)} %copy-done.3, f32[512]{0:T(512)S(1)} %copy-done.8, f32[512]{0:T(512)S(1)} %copy-done.9, f32[2048]{0:T(1024)S(1)} %add_rsqrt_fusion, f32[2048]{0:T(1024)S(1)} %broadcast_multiply_fusion, ...), kind=kOutput, calls=%fused_computation.19 | convolution fusion | flops 344342528 | bytes 6486016 | tf_op jit(solution)/shard_map/dot_general | solution.py:106
  136.8 7.2 %all-gather = bf16[640,512]{1,0:T(8,128)(2,1)S(1)} all-gather(bf16[160,512]{1,0:T(8,128)(2,1)S(1)} %fusion.9), channel_id=2, replica_groups=mesh['band'=8,'feat'=4] {'feat'}, dimensions={0}, use_global_device_ids=true | all-gather | bytes 819200 | tf_op jit(solution)/shard_map/all_gather | solution.py:11
  144.1 1.8 %fusion.31 = (f32[160]{0:T(256)S(1)}, f32[160,512]{1,0:T(8,128)S(1)}) fusion(f32[512]{0:T(512)S(1)} %copy-done.10, bf16[512,512]{1,0:T(8,128)(2,1)} %param.32, f32[160,512]{1,0:T(8,128)S(1)} %fusion.18, bf16[160,512]{1,0:T(8,128)(2,1)S(1)} %reduce_sum.50, bf16[1024,512]{1,0:T(8,128)(2,1)} %param.30, f32[512]{0:T(512)S(1)} %copy-done.11), kind=kOutput, calls=%fused_computation.46 | convolution fusion | flops 168509280 | bytes 1872512 | tf_op jit(solution)/shard_map/dot_general | solution.py:33
  (57 shorter events, 8.7 us)
Async XLA Ops:
  0.0 132.2 %copy-start = (bf16[512,512]{1,0:T(8,128)(2,1)S(1)}, bf16[512,512]{1,0:T(8,128)(2,1)}, u32[]{:S(2)}) copy-start(bf16[512,512]{1,0:T(8,128)(2,1)} %param.26) | copy-start | bytes 1572868
  64.8 11.0 %copy-start.1 = (bf16[1,1,2048,512]{3,2,1,0:T(8,128)(2,1)S(1)}, bf16[1,1,2048,512]{3,2,1,0:T(8,128)(2,1)}, u32[]{:S(2)}) copy-start(bf16[1,1,2048,512]{3,2,1,0:T(8,128)(2,1)} %param.21) | copy-start | bytes 6291460
  69.3 10.5 %copy-start.4 = (bf16[160,128]{1,0:T(8,128)(2,1)S(1)}, bf16[160,128]{1,0:T(8,128)(2,1)}, u32[]{:S(2)}) copy-start(bf16[160,128]{1,0:T(8,128)(2,1)} %param.20) | copy-start | bytes 122884
  69.3 16.2 %copy-start.5 = (s32[1,1,2048]{2,1,0:T(1,128)S(1)}, s32[1,1,2048]{2,1,0:T(1,128)}, u32[]{:S(2)}) copy-start(s32[1,1,2048]{2,1,0:T(1,128)} %param.23) | copy-start | bytes 24580
  69.3 54.5 %all-to-all-start.1 = ((bf16[8,256,512]{1,2,0:T(8,128)(2,1)}), bf16[8,256,512]{1,2,0:T(8,128)(2,1)}, u32[]{:S(2)}, u32[]{:S(2)}) async-start(bf16[8,256,512]{1,2,0:T(8,128)(2,1)} %bitcast.37), calls=%async_computation.1 | async-start | bytes 4194304 | tf_op jit(solution)/shard_map/all_to_all | solution.py:78
  126.6 2.5 %copy-start.2 = (f32[2048,512]{1,0:T(8,128)S(1)}, f32[2048,512]{1,0:T(8,128)}, u32[]{:S(2)}) copy-start(f32[2048,512]{1,0:T(8,128)} %fusion.5) | copy-start | bytes 12582916
  126.7 2.5 %copy-start.7 = (f32[512]{0:T(512)S(1)}, f32[512]{0:T(512)}, u32[]{:S(2)}) copy-start(f32[512]{0:T(512)} %param.25) | copy-start | bytes 6148
  129.1 3.1 %copy-start.6 = (f32[512]{0:T(512)S(1)}, f32[512]{0:T(512)}, u32[]{:S(2)}) copy-start(f32[512]{0:T(512)} %param.27) | copy-start | bytes 6148
  133.6 1.6 %copy-start.3 = (bf16[1,1,2048,512]{2,3,1,0:T(8,128)(2,1)S(1)}, bf16[1,1,2048,512]{2,3,1,0:T(8,128)(2,1)}, u32[]{:S(2)}) copy-start(bf16[1,1,2048,512]{2,3,1,0:T(8,128)(2,1)} %copy.27) | copy-start | bytes 6291460
  133.6 1.6 %copy-start.8 = (f32[512]{0:T(512)S(1)}, f32[512]{0:T(512)}, u32[]{:S(2)}) copy-start(f32[512]{0:T(512)} %param.29) | copy-start | bytes 6148
  133.6 1.6 %copy-start.9 = (f32[512]{0:T(512)S(1)}, f32[512]{0:T(512)}, u32[]{:S(2)}) copy-start(f32[512]{0:T(512)} %param.28) | copy-start | bytes 6148
  135.2 8.9 %copy-start.10 = (f32[512]{0:T(512)S(1)}, f32[512]{0:T(512)}, u32[]{:S(2)}) copy-start(f32[512]{0:T(512)} %param.33) | copy-start | bytes 6148
  135.2 8.9 %copy-start.11 = (f32[512]{0:T(512)S(1)}, f32[512]{0:T(512)}, u32[]{:S(2)}) copy-start(f32[512]{0:T(512)} %param.31) | copy-start | bytes 6148
